TPU v7x, 32 devices: a whole 2x2x4 slice. The times are simulated.
32 devices in a mesh: row: 4 (over y, x), col: 8 (over z, core).
Axes of the slice: x: 2, y: 2, z: 4, core: 2. Of those that a mesh axis runs over, the one named last changes fastest.
Arguments:
- coeffs: bfloat16 [16384, 2048], P('row'), may hold values from -1 to 1
- p_slots: int32 [4, 8, 64], P('row', 'col'), may hold values from 0 to 511, as said below
- p_count: int32 [4, 8], P('row', 'col'), may hold values from 1 to 64
- s_blocks: bfloat16 [4, 8, 64, 128, 128], P('row', 'col'), may hold values from -0.3984375 to 0.3984375
- s_slots: int32 [4, 8, 64], P('row', 'col'), may hold values from 0 to 511, as said below
- s_count: int32 [4, 8], P('row', 'col'), may hold values from 1 to 64
- q_slots: int32 [4, 8, 64], P('row', 'col'), may hold values from 0 to 511, as said below
- q_count: int32 [4, 8], P('row', 'col'), may hold values from 1 to 64
Outputs:
- density: bfloat16 [4, 8, 64, 128, 128], P('row', 'col')
- product: float32 [4, 8, 64, 128, 128], P('row', 'col')
Inputs may be any that keep to these rules, and one draw needn't show every extreme that they name: `p_slots`: on each device the live slots name different blocks of its tile; at least one device has all 64 slots live, which one is drawn. `s_slots`: on each device the live slots name different positions; at least one device has all 64 slots live, which one is drawn. `q_slots`: on each device the live slots name different blocks of its tile; at least one device has all 64 slots live, which one is drawn.
All inputs are finite; a program needn't handle non-finite values.
Results may differ from a plain program's by a relative error of at most 0.0029.
Values may be sent and summed in bfloat16 or wider, within the bound.
A program may use at most 192 MiB of HBM per device.

v0:
```python
import jax
import jax.numpy as jnp
from jax import lax
from jax.sharding import PartitionSpec as P


def from_root(block, axis, source):
    block = jnp.where(lax.axis_index(axis) == source, block, jnp.zeros_like(block))
    return lax.psum(block, axis)


def shortened(shard):

    def short(part):
        return part.astype(jnp.bfloat16) if part.dtype == jnp.float32 else part

    return jax.tree.map(short, shard)


def shifted(block, axis, distance):
    devices = range(lax.axis_size(axis))
    route = [((i - distance) % len(devices), i) for i in devices]
    return lax.ppermute(block, axis, route)


def step_product(summed, p_data, s_data, panel_slot, q_row, q_col, tile_cols):
    p_blocks, p_code = p_data
    s_blocks, s_code = s_data
    local_k = jnp.arange(tile_cols, dtype=jnp.int32)
    p_live = p_code >= 0
    p_row = jnp.where(p_live, p_code // tile_cols, -1)
    p_col = jnp.where(p_live, p_code % tile_cols, -1)
    pick_left = (
        (p_row[:, None, None] == q_row[None, :, None])
        & (p_col[:, None, None] == local_k[None, None, :])
    ).astype(jnp.bfloat16)
    left_rows = jnp.einsum("pqk,pab->qakb", pick_left, p_blocks, preferred_element_type=jnp.float32)
    left_rows = left_rows.astype(jnp.bfloat16).reshape(q_row.shape[0], 128, tile_cols * 128)
    square = tile_cols * tile_cols
    s_live = (s_code >= 0) & (s_code // square == panel_slot)
    s_local = s_code % square
    s_row = jnp.where(s_live, s_local // tile_cols, -1)
    s_col = s_local % tile_cols
    pick_right = (
        (s_row[:, None, None] == local_k[None, :, None])
        & (s_col[:, None, None] == q_col[None, None, :])
    ).astype(jnp.bfloat16)
    right_cols = jnp.einsum(
        "skq,sab->kaqb", pick_right, s_blocks, preferred_element_type=jnp.float32
    )
    right_cols = right_cols.astype(jnp.bfloat16).reshape(tile_cols * 128, q_row.shape[0], 128)
    return summed + jnp.einsum(
        "qak,kqb->qab", left_rows, right_cols, preferred_element_type=jnp.float32
    )


def pick_tree(flag, moved, kept):
    return jax.tree.map(lambda fresh, stale: jnp.where(flag, fresh, stale), moved, kept)


def on_device(coeffs, p_slots, p_count, s_blocks, s_slots, s_count, q_slots, q_count):
    rows_n = lax.axis_size("row")
    cols_n = lax.axis_size("col")
    row_at = lax.axis_index("row")
    col_at = lax.axis_index("col")
    panel_rows, orbitals = coeffs.shape
    tile_rows = panel_rows // 128
    tile_cols = panel_rows * rows_n // cols_n // 128
    sub_span = cols_n // rows_n
    source = from_root(coeffs, "row", col_at // sub_span)
    column_rows = lax.dynamic_slice_in_dim(
        source, col_at % sub_span * (tile_cols * 128), tile_cols * 128, 0
    )
    slot_ids = p_slots[0, 0]
    p_max = slot_ids.shape[0]
    p_live = jnp.arange(p_max, dtype=jnp.int32) < p_count[0, 0]
    left = coeffs.reshape(tile_rows, 128, orbitals)[slot_ids // tile_cols]
    right = column_rows.reshape(tile_cols, 128, orbitals)[slot_ids % tile_cols]
    raw = jnp.einsum("pak,pbk->pab", left, right, preferred_element_type=jnp.float32)
    dense_blocks = jnp.where(p_live[:, None, None], raw, jnp.zeros_like(raw)).astype(jnp.bfloat16)
    p_code = jnp.where(p_live, slot_ids, -1)
    s_ids = s_slots[0, 0]
    s_max = s_ids.shape[0]
    s_live = jnp.arange(s_max, dtype=jnp.int32) < s_count[0, 0]
    s_code = jnp.where(s_live, s_ids, -1)
    s_local = s_blocks[0, 0]
    q_ids = q_slots[0, 0]
    q_max = q_ids.shape[0]
    q_live = jnp.arange(q_max, dtype=jnp.int32) < q_count[0, 0]
    q_row = q_ids // tile_cols
    q_col = q_ids % tile_cols
    zeros_out = jnp.zeros((q_max, 128, 128), jnp.float32)
    p_data = (dense_blocks, p_code)
    s_data = (s_local, s_code)
    level_count = rows_n.bit_length() - 1
    for level in range(level_count):
        moved = jax.tree.map(
            lambda part, own: part.astype(own.dtype),
            shifted(shortened(p_data), "col", -(1 << level)),
            p_data,
        )
        p_data = pick_tree(row_at >> level & 1 == 1, moved, p_data)
    row_offset = col_at % rows_n
    for level in range(level_count):
        moved = jax.tree.map(
            lambda part, own: part.astype(own.dtype),
            shifted(shortened(s_data), "row", -(1 << level)),
            s_data,
        )
        s_data = pick_tree(row_offset >> level & 1 == 1, moved, s_data)

    def advance(step_at, carry):
        summed, p_held, s_held = carry
        panel_at = (row_at + col_at + step_at) % cols_n
        summed = step_product(summed, p_held, s_held, panel_at // rows_n, q_row, q_col, tile_cols)
        p_held = jax.tree.map(
            lambda part, own: part.astype(own.dtype), shifted(shortened(p_held), "col", -1), p_held
        )
        s_held = jax.tree.map(
            lambda part, own: part.astype(own.dtype), shifted(shortened(s_held), "row", -1), s_held
        )
        return (summed, p_held, s_held)

    summed, p_data, s_data = lax.fori_loop(0, cols_n - 1, advance, (zeros_out, p_data, s_data))
    panel_at = (row_at + col_at + cols_n - 1) % cols_n
    summed = step_product(summed, p_data, s_data, panel_at // rows_n, q_row, q_col, tile_cols)
    product = jnp.where(q_live[:, None, None], summed, jnp.zeros_like(summed))
    return (dense_blocks.reshape(1, 1, p_max, 128, 128), product.reshape(1, 1, q_max, 128, 128))


def solution(mesh):
    return jax.shard_map(
        on_device,
        mesh=mesh,
        in_specs=(
            P("row", None),
            P("row", "col", None),
            P("row", "col"),
            P("row", "col", None, None, None),
            P("row", "col", None),
            P("row", "col"),
            P("row", "col", None),
            P("row", "col"),
        ),
        out_specs=(P("row", "col", None, None, None), P("row", "col", None, None, None)),
        check_vma=False,
    )
```

profile of v0, /device:TPU:0, one launch (start us, length us, event | category | flops | bytes accessed | tf_op | source)
XLA Modules:
  0.0 1880.4 jit_solution(13841358631608636264)
XLA Ops:
  7.2 13.8 broadcast_select_fusion
  22.6 2.7 copy.34
  26.0 19.3 %gather_fusion = bf16[64,128,2048]{2,1,0:T(8,128)(2,1)} fusion(bf16[32,128,2048]{2,1,0:T(8,128)(2,1)} %bitcast.130, s32[1024]{0:T(1024)S(1)} %get-tuple-element.386), kind=kCustom, calls=%fused_computation | custom fusion | bytes 67109120 | tf_op jit(solution)/shard_map/gather | solution.py:77
  45.3 329.8 %all-reduce.2.cloned.1.call-done = bf16[4096,2048]{1,0:T(8,128)(2,1)} async-done(((bf16[4096,2048]{1,0:T(8,128)(2,1)}), bf16[4096,2048]{1,0:T(8,128)(2,1)}) %all-reduce.2.cloned.1.call-update) | async-done | bytes 16777232 | tf_op jit(solution)/shard_map/psum | solution.py:9
  375.1 8.3 constant_dynamic-slice_fusion
  383.4 15.8 gather_fusion.1
  399.2 24.5 %select_convert_fusion = bf16[64,128,128]{2,1,0:T(8,128)(2,1)} fusion(pred[64]{0:T(512)(128)(4,1)S(1)} %iota_compare_fusion.5, bf16[64,128,2048]{2,1,0:T(8,128)(2,1)} %gather_fusion, bf16[64,128,2048]{2,1,0:T(8,128)(2,1)} %gather_fusion.1), kind=kOutput, calls=%fused_computation.45 | convolution fusion | flops 4297064448 | bytes 69206080 | tf_op jit(solution)/shard_map/pak,pbk->pab/dot_general | solution.py:79
  423.8 2.7 collective-permute-start.4
  426.4 3.1 broadcast_select_fusion.1
  431.3 19.0 %collective-permute-done.4 = bf16[64,128,128]{2,1,0:T(8,128)(2,1)} collective-permute-done((bf16[64,128,128]{2,1,0:T(8,128)(2,1)}, bf16[64,128,128]{2,1,0:T(8,128)(2,1)}, u32[]{:S(2)}, u32[]{:S(2)}) %collective-permute-start.4) | collective-permute-done | bytes 2097184 | tf_op jit(solution)/shard_map/ppermute | solution.py:23
  450.3 3.1 broadcast_select_fusion.3
  454.2 3.0 collective-permute-start.6
  457.9 2.6 collective-permute-start.10
  462.3 35.8 %collective-permute-done.6 = s32[64]{0:T(128)S(1)} collective-permute-done((s32[64]{0:T(128)S(1)}, s32[64]{0:T(128)S(1)}, u32[]{:S(2)}, u32[]{:S(2)}) %collective-permute-start.6) | collective-permute-done | bytes 288 | tf_op jit(solution)/shard_map/ppermute | solution.py:23
  503.9 1.8 broadcast_select_fusion.4
  505.7 2.7 copy.15
  508.4 1178.7 %while.25 = (s32[]{:T(128)}, f32[64,128,128]{2,1,0:T(8,128)}, bf16[64,128,128]{2,0,1:T(8,128)(2,1)}, s32[64]{0:T(128)S(1)}, bf16[64,128,128]{2,0,1:T(8,128)(2,1)...) while((s32[]{:T(128)}, f32[64,128,128]{2,1,0:T(8,128)}, ...), condition=%wide.region_2.3_spmd.clone, body=%wide.region_1.2_spmd.clone.sunk | while | flops 8625731584 | bytes 239103024 | solution.py:124
  510.1 5.6 collective-permute-start
  515.7 3.1 copy.48
  518.9 2.6 collective-permute-start.2
  522.1 13.8 convert_bitcast_fusion.4
  536.0 49.3 %reshape.448 = bf16[64,128,2048]{2,1,0:T(8,128)(2,1)} reshape(bf16[64,128,16,128]{3,2,1,0:T(8,128)(2,1)} %convert_bitcast_fusion.4) | data formatting | bytes 67108864 | tf_op jit(solution)/shard_map/while/body/eval_jaxpr/reshape | solution.py:38
  585.2 15.5 convolution_convert_fusion.2
  600.8 79.3 %select_add_fusion.2 = f32[64,128,128]{2,1,0:T(8,128)} fusion(f32[64,128,128]{2,1,0:T(8,128)} %get-tuple-element.471, pred[]{:T(512)S(6)} %compare.95, bf16[64,128,2048]{2,1,0:T(8,128)(2,1)} %reshape.448, bf16[2048,64,128]{2,1,0:T(8,128)(2,1)} %bitcast.128), kind=kOutput, calls=%fused_computation.6.clone.1 | convolution fusion | flops 4297064448 | bytes 75497472 | tf_op jit(solution)/shard_map/while/body/eval_jaxpr/qak,kqb->qab/dot_general | solution.py:52
  681.7 3.1 copy.48
  687.0 13.9 convert_bitcast_fusion.4
  700.8 49.3 %reshape.448 = bf16[64,128,2048]{2,1,0:T(8,128)(2,1)} reshape(bf16[64,128,16,128]{3,2,1,0:T(8,128)(2,1)} %convert_bitcast_fusion.4) | data formatting | bytes 67108864 | tf_op jit(solution)/shard_map/while/body/eval_jaxpr/reshape | solution.py:38
  750.1 15.5 convolution_convert_fusion.2
  765.6 80.5 %select_add_fusion.2 = f32[64,128,128]{2,1,0:T(8,128)} fusion(f32[64,128,128]{2,1,0:T(8,128)} %get-tuple-element.471, pred[]{:T(512)S(6)} %compare.95, bf16[64,128,2048]{2,1,0:T(8,128)(2,1)} %reshape.448, bf16[2048,64,128]{2,1,0:T(8,128)(2,1)} %bitcast.128), kind=kOutput, calls=%fused_computation.6.clone.1 | convolution fusion | flops 4297064448 | bytes 75497472 | tf_op jit(solution)/shard_map/while/body/eval_jaxpr/qak,kqb->qab/dot_general | solution.py:52
  849.2 3.1 copy.48
  852.3 2.6 collective-permute-start.2
  855.6 13.8 convert_bitcast_fusion.4
  869.5 49.3 %reshape.448 = bf16[64,128,2048]{2,1,0:T(8,128)(2,1)} reshape(bf16[64,128,16,128]{3,2,1,0:T(8,128)(2,1)} %convert_bitcast_fusion.4) | data formatting | bytes 67108864 | tf_op jit(solution)/shard_map/while/body/eval_jaxpr/reshape | solution.py:38
  918.8 15.5 convolution_convert_fusion.2
  934.3 80.5 %select_add_fusion.2 = f32[64,128,128]{2,1,0:T(8,128)} fusion(f32[64,128,128]{2,1,0:T(8,128)} %get-tuple-element.471, pred[]{:T(512)S(6)} %compare.95, bf16[64,128,2048]{2,1,0:T(8,128)(2,1)} %reshape.448, bf16[2048,64,128]{2,1,0:T(8,128)(2,1)} %bitcast.128), kind=kOutput, calls=%fused_computation.6.clone.1 | convolution fusion | flops 4297064448 | bytes 75497472 | tf_op jit(solution)/shard_map/while/body/eval_jaxpr/qak,kqb->qab/dot_general | solution.py:52
  1016.6 3.1 copy.48
  1021.8 13.9 convert_bitcast_fusion.4
  1035.7 49.3 %reshape.448 = bf16[64,128,2048]{2,1,0:T(8,128)(2,1)} reshape(bf16[64,128,16,128]{3,2,1,0:T(8,128)(2,1)} %convert_bitcast_fusion.4) | data formatting | bytes 67108864 | tf_op jit(solution)/shard_map/while/body/eval_jaxpr/reshape | solution.py:38
  1085.0 15.5 convolution_convert_fusion.2
  1100.5 80.5 %select_add_fusion.2 = f32[64,128,128]{2,1,0:T(8,128)} fusion(f32[64,128,128]{2,1,0:T(8,128)} %get-tuple-element.471, pred[]{:T(512)S(6)} %compare.95, bf16[64,128,2048]{2,1,0:T(8,128)(2,1)} %reshape.448, bf16[2048,64,128]{2,1,0:T(8,128)(2,1)} %bitcast.128), kind=kOutput, calls=%fused_computation.6.clone.1 | convolution fusion | flops 4297064448 | bytes 75497472 | tf_op jit(solution)/shard_map/while/body/eval_jaxpr/qak,kqb->qab/dot_general | solution.py:52
  1184.1 2.3 collective-permute-start.1
  1186.4 3.1 copy.48
  1189.5 2.6 collective-permute-start.2
  1192.7 13.9 convert_bitcast_fusion.4
  1206.6 49.3 %reshape.448 = bf16[64,128,2048]{2,1,0:T(8,128)(2,1)} reshape(bf16[64,128,16,128]{3,2,1,0:T(8,128)(2,1)} %convert_bitcast_fusion.4) | data formatting | bytes 67108864 | tf_op jit(solution)/shard_map/while/body/eval_jaxpr/reshape | solution.py:38
  1255.9 15.5 convolution_convert_fusion.2
  1271.4 80.5 %select_add_fusion.2 = f32[64,128,128]{2,1,0:T(8,128)} fusion(f32[64,128,128]{2,1,0:T(8,128)} %get-tuple-element.471, pred[]{:T(512)S(6)} %compare.95, bf16[64,128,2048]{2,1,0:T(8,128)(2,1)} %reshape.448, bf16[2048,64,128]{2,1,0:T(8,128)(2,1)} %bitcast.128), kind=kOutput, calls=%fused_computation.6.clone.1 | convolution fusion | flops 4297064448 | bytes 75497472 | tf_op jit(solution)/shard_map/while/body/eval_jaxpr/qak,kqb->qab/dot_general | solution.py:52
  1353.6 3.1 copy.48
  1358.8 13.8 convert_bitcast_fusion.4
  1372.6 49.3 %reshape.448 = bf16[64,128,2048]{2,1,0:T(8,128)(2,1)} reshape(bf16[64,128,16,128]{3,2,1,0:T(8,128)(2,1)} %convert_bitcast_fusion.4) | data formatting | bytes 67108864 | tf_op jit(solution)/shard_map/while/body/eval_jaxpr/reshape | solution.py:38
  1421.9 15.5 convolution_convert_fusion.2
  1437.5 80.5 %select_add_fusion.2 = f32[64,128,128]{2,1,0:T(8,128)} fusion(f32[64,128,128]{2,1,0:T(8,128)} %get-tuple-element.471, pred[]{:T(512)S(6)} %compare.95, bf16[64,128,2048]{2,1,0:T(8,128)(2,1)} %reshape.448, bf16[2048,64,128]{2,1,0:T(8,128)(2,1)} %bitcast.128), kind=kOutput, calls=%fused_computation.6.clone.1 | convolution fusion | flops 4297064448 | bytes 75497472 | tf_op jit(solution)/shard_map/while/body/eval_jaxpr/qak,kqb->qab/dot_general | solution.py:52
  1521.0 3.1 copy.48
  1524.1 2.6 collective-permute-start.2
  1527.5 13.8 convert_bitcast_fusion.4
  1541.3 49.3 %reshape.448 = bf16[64,128,2048]{2,1,0:T(8,128)(2,1)} reshape(bf16[64,128,16,128]{3,2,1,0:T(8,128)(2,1)} %convert_bitcast_fusion.4) | data formatting | bytes 67108864 | tf_op jit(solution)/shard_map/while/body/eval_jaxpr/reshape | solution.py:38
  1590.6 15.5 convolution_convert_fusion.2
  1606.1 80.5 %select_add_fusion.2 = f32[64,128,128]{2,1,0:T(8,128)} fusion(f32[64,128,128]{2,1,0:T(8,128)} %get-tuple-element.471, pred[]{:T(512)S(6)} %compare.95, bf16[64,128,2048]{2,1,0:T(8,128)(2,1)} %reshape.448, bf16[2048,64,128]{2,1,0:T(8,128)(2,1)} %bitcast.128), kind=kOutput, calls=%fused_computation.6.clone.1 | convolution fusion | flops 4297064448 | bytes 75497472 | tf_op jit(solution)/shard_map/while/body/eval_jaxpr/qak,kqb->qab/dot_general | solution.py:52
  1687.2 15.6 convert_bitcast_fusion.2
  1702.7 47.4 %copy.16 = bf16[64,128,16,128]{1,3,2,0:T(8,128)(2,1)} copy(bf16[64,128,16,128]{3,0,2,1:T(8,128)(2,1)} %convert_bitcast_fusion.2) | data formatting | bytes 67108864 | tf_op jit(solution)/shard_map/convert_element_type | solution.py:38
  1750.3 15.6 convert_bitcast_fusion.1
  1765.9 23.1 %copy.17 = bf16[16,128,64,128]{3,2,1,0:T(8,128)(2,1)} copy(bf16[16,128,64,128]{3,2,0,1:T(8,128)(2,1)} %convert_bitcast_fusion.1) | data formatting | bytes 67108864 | tf_op jit(solution)/shard_map/convert_element_type | solution.py:51
  1789.0 78.4 %fusion.14 = f32[64,128,128]{2,1,0:T(8,128)} fusion(bf16[64,128,2048]{1,2,0:T(8,128)(2,1)} %bitcast.131, bf16[2048,64,128]{2,1,0:T(8,128)(2,1)} %bitcast.132), kind=kOutput, calls=%fused_computation.39 | convolution fusion | flops 4294967296 | bytes 71303168 | tf_op jit(solution)/shard_map/qak,kqb->qab/dot_general | solution.py:52
  1867.4 5.9 select_bitcast_fusion
  (159 shorter events, 35.4 us)
Async XLA Ops:
  7.2 367.9 %all-reduce.2.cloned.1.call-start = ((), (), s32[]{:S(2)}) async-start(), calls=%async_computation | async-start | bytes 33554432 | tf_op jit(solution)/shard_map/psum | solution.py:9
  21.0 1.6 copy-start
  22.6 3.3 copy-start.2
  25.3 401.2 %collective-permute-start.8 = (bf16[64,128,128]{2,0,1:T(8,128)(2,1)}, bf16[64,128,128]{2,0,1:T(8,128)(2,1)}, u32[]{:S(2)}, u32[]{:S(2)}) collective-permute-start(bf16[64,128,128]{2,0,1:T(8,128)(2,1)} %bitcast.107), channel_id=1, source_target_pairs={{8,0},{16,8},{24,16},{0,24},{9,1},{17,9},{25,17},{1,25},{10,2},{18... | collective-permute-start | bytes 6291464 | tf_op jit(solution)/shard_map/ppermute | solution.py:23
  423.8 26.5 %collective-permute-start.4 = (bf16[64,128,128]{2,1,0:T(8,128)(2,1)}, bf16[64,128,128]{2,1,0:T(8,128)(2,1)}, u32[]{:S(2)}, u32[]{:S(2)}) collective-permute-start(bf16[64,128,128]{2,1,0:T(8,128)(2,1)} %select_convert_fusion), channel_id=1, source_target_pairs={{1,0},{2,1},{3,2},{4,3},{5,4},{6,5},{7,6},{0,7},{9,8},{10,9},{11,1... | collective-permute-start | bytes 6291464 | tf_op jit(solution)/shard_map/ppermute | solution.py:23
  429.6 28.3 %copy-start.3 = (s32[1,1,64]{2,1,0:T(1,128)S(1)}, s32[1,1,64]{2,1,0:T(1,128)}, u32[]{:S(2)}) copy-start(s32[1,1,64]{2,1,0:T(1,128)} %param.14) | copy-start | bytes 772
  429.6 32.1 %copy-start.5 = (s32[1,1,64]{2,1,0:T(1,128)S(1)}, s32[1,1,64]{2,1,0:T(1,128)}, u32[]{:S(2)}) copy-start(s32[1,1,64]{2,1,0:T(1,128)} %param.16) | copy-start | bytes 772
  429.6 72.7 %collective-permute-start.9 = (bf16[64,128,128]{2,0,1:T(8,128)(2,1)S(1)}, bf16[64,128,128]{2,0,1:T(8,128)(2,1)}, u32[]{:S(2)}, u32[]{:S(2)}) collective-permute-start(bf16[64,128,128]{2,0,1:T(8,128)(2,1)S(1)} %broadcast_select_fusion.1), channel_id=1, source_target_pairs={{16,0},{24,8},{0,16},{8,24},{17,1},{25,9},{1,17},{9,25},{18,2},{26... | collective-permute-start | bytes 6291464 | tf_op jit(solution)/shard_map/ppermute | solution.py:23
  453.4 50.4 %collective-permute-start.5 = (bf16[64,128,128]{2,1,0:T(8,128)(2,1)}, bf16[64,128,128]{2,1,0:T(8,128)(2,1)}, u32[]{:S(2)}, u32[]{:S(2)}) collective-permute-start(bf16[64,128,128]{2,1,0:T(8,128)(2,1)} %broadcast_select_fusion.3), channel_id=1, source_target_pairs={{2,0},{3,1},{4,2},{5,3},{6,4},{7,5},{0,6},{1,7},{10,8},{11,9},{12,... | collective-permute-start | bytes 6291464 | tf_op jit(solution)/shard_map/ppermute | solution.py:23
  454.2 43.9 %collective-permute-start.6 = (s32[64]{0:T(128)S(1)}, s32[64]{0:T(128)S(1)}, u32[]{:S(2)}, u32[]{:S(2)}) collective-permute-start(s32[64]{0:T(128)S(1)} %bitcast_select_fusion), channel_id=1, source_target_pairs={{1,0},{2,1},{3,2},{4,3},{5,4},{6,5},{7,6},{0,7},{9,8},{10,9},{11,1... | collective-permute-start | bytes 776 | tf_op jit(solution)/shard_map/ppermute | solution.py:23
  457.9 40.8 %collective-permute-start.10 = (s32[64]{0:T(128)S(1)}, s32[64]{0:T(128)S(1)}, u32[]{:S(2)}, u32[]{:S(2)}) collective-permute-start(s32[64]{0:T(128)S(1)} %compare_select_fusion.15), channel_id=1, source_target_pairs={{8,0},{16,8},{24,16},{0,24},{9,1},{17,9},{25,17},{1,25},{10,2},{18... | collective-permute-start | bytes 776 | tf_op jit(solution)/shard_map/ppermute | solution.py:23
  498.1 3.7 collective-permute-start.7
  498.7 3.6 collective-permute-start.11
  510.1 170.0 %collective-permute-start = (bf16[64,128,128]{2,0,1:T(8,128)(2,1)S(1)}, bf16[64,128,128]{2,0,1:T(8,128)(2,1)}, u32[]{:S(2)}, u32[]{:S(2)}) collective-permute-start(bf16[64,128,128]{2,0,1:T(8,128)(2,1)S(1)} %copy.46), channel_id=1, source_target_pairs={{1,0},{2,1},{3,2},{4,3},{5,4},{6,5},{7,6},{0,7},{9,8},{10,9},{11,1... | collective-permute-start | bytes 6291464 | tf_op jit(solution)/shard_map/while/body/eval_jaxpr/ppermute | solution.py:23
  515.7 164.4 %collective-permute-start.1 = (s32[64]{0:T(128)S(1)}, s32[64]{0:T(128)S(1)}, u32[]{:S(2)}, u32[]{:S(2)}) collective-permute-start(s32[64]{0:T(128)S(1)} %copy.47), channel_id=1, source_target_pairs={{1,0},{2,1},{3,2},{4,3},{5,4},{6,5},{7,6},{0,7},{9,8},{10,9},{11,1... | collective-permute-start | bytes 776 | tf_op jit(solution)/shard_map/while/body/eval_jaxpr/ppermute | solution.py:23
  518.9 161.2 %collective-permute-start.2 = (bf16[64,128,128]{2,0,1:T(8,128)(2,1)}, bf16[64,128,128]{2,0,1:T(8,128)(2,1)}, u32[]{:S(2)}, u32[]{:S(2)}) collective-permute-start(bf16[64,128,128]{2,0,1:T(8,128)(2,1)} %copy.48), channel_id=1, source_target_pairs={{8,0},{16,8},{24,16},{0,24},{9,1},{17,9},{25,17},{1,25},{10,2},{18... | collective-permute-start | bytes 6291464 | tf_op jit(solution)/shard_map/while/body/eval_jaxpr/ppermute | solution.py:23
  521.4 158.6 %collective-permute-start.3 = (s32[64]{0:T(128)S(1)}, s32[64]{0:T(128)S(1)}, u32[]{:S(2)}, u32[]{:S(2)}) collective-permute-start(s32[64]{0:T(128)S(1)} %copy.49), channel_id=1, source_target_pairs={{8,0},{16,8},{24,16},{0,24},{9,1},{17,9},{25,17},{1,25},{10,2},{18... | collective-permute-start | bytes 776 | tf_op jit(solution)/shard_map/while/body/eval_jaxpr/ppermute | solution.py:23
  681.7 164.4 %collective-permute-start = (bf16[64,128,128]{2,0,1:T(8,128)(2,1)S(1)}, bf16[64,128,128]{2,0,1:T(8,128)(2,1)}, u32[]{:S(2)}, u32[]{:S(2)}) collective-permute-start(bf16[64,128,128]{2,0,1:T(8,128)(2,1)S(1)} %copy.46), channel_id=1, source_target_pairs={{1,0},{2,1},{3,2},{4,3},{5,4},{6,5},{7,6},{0,7},{9,8},{10,9},{11,1... | collective-permute-start | bytes 6291464 | tf_op jit(solution)/shard_map/while/body/eval_jaxpr/ppermute | solution.py:23
  681.7 164.4 %collective-permute-start.1 = (s32[64]{0:T(128)S(1)}, s32[64]{0:T(128)S(1)}, u32[]{:S(2)}, u32[]{:S(2)}) collective-permute-start(s32[64]{0:T(128)S(1)} %copy.47), channel_id=1, source_target_pairs={{1,0},{2,1},{3,2},{4,3},{5,4},{6,5},{7,6},{0,7},{9,8},{10,9},{11,1... | collective-permute-start | bytes 776 | tf_op jit(solution)/shard_map/while/body/eval_jaxpr/ppermute | solution.py:23
  684.8 161.3 %collective-permute-start.2 = (bf16[64,128,128]{2,0,1:T(8,128)(2,1)}, bf16[64,128,128]{2,0,1:T(8,128)(2,1)}, u32[]{:S(2)}, u32[]{:S(2)}) collective-permute-start(bf16[64,128,128]{2,0,1:T(8,128)(2,1)} %copy.48), channel_id=1, source_target_pairs={{8,0},{16,8},{24,16},{0,24},{9,1},{17,9},{25,17},{1,25},{10,2},{18... | collective-permute-start | bytes 6291464 | tf_op jit(solution)/shard_map/while/body/eval_jaxpr/ppermute | solution.py:23
  686.3 159.8 %collective-permute-start.3 = (s32[64]{0:T(128)S(1)}, s32[64]{0:T(128)S(1)}, u32[]{:S(2)}, u32[]{:S(2)}) collective-permute-start(s32[64]{0:T(128)S(1)} %copy.49), channel_id=1, source_target_pairs={{8,0},{16,8},{24,16},{0,24},{9,1},{17,9},{25,17},{1,25},{10,2},{18... | collective-permute-start | bytes 776 | tf_op jit(solution)/shard_map/while/body/eval_jaxpr/ppermute | solution.py:23
  847.7 167.1 %collective-permute-start = (bf16[64,128,128]{2,0,1:T(8,128)(2,1)S(1)}, bf16[64,128,128]{2,0,1:T(8,128)(2,1)}, u32[]{:S(2)}, u32[]{:S(2)}) collective-permute-start(bf16[64,128,128]{2,0,1:T(8,128)(2,1)S(1)} %copy.46), channel_id=1, source_target_pairs={{1,0},{2,1},{3,2},{4,3},{5,4},{6,5},{7,6},{0,7},{9,8},{10,9},{11,1... | collective-permute-start | bytes 6291464 | tf_op jit(solution)/shard_map/while/body/eval_jaxpr/ppermute | solution.py:23
  848.0 166.8 %collective-permute-start.1 = (s32[64]{0:T(128)S(1)}, s32[64]{0:T(128)S(1)}, u32[]{:S(2)}, u32[]{:S(2)}) collective-permute-start(s32[64]{0:T(128)S(1)} %copy.47), channel_id=1, source_target_pairs={{1,0},{2,1},{3,2},{4,3},{5,4},{6,5},{7,6},{0,7},{9,8},{10,9},{11,1... | collective-permute-start | bytes 776 | tf_op jit(solution)/shard_map/while/body/eval_jaxpr/ppermute | solution.py:23
  852.3 162.5 %collective-permute-start.2 = (bf16[64,128,128]{2,0,1:T(8,128)(2,1)}, bf16[64,128,128]{2,0,1:T(8,128)(2,1)}, u32[]{:S(2)}, u32[]{:S(2)}) collective-permute-start(bf16[64,128,128]{2,0,1:T(8,128)(2,1)} %copy.48), channel_id=1, source_target_pairs={{8,0},{16,8},{24,16},{0,24},{9,1},{17,9},{25,17},{1,25},{10,2},{18... | collective-permute-start | bytes 6291464 | tf_op jit(solution)/shard_map/while/body/eval_jaxpr/ppermute | solution.py:23
  855.0 159.9 %collective-permute-start.3 = (s32[64]{0:T(128)S(1)}, s32[64]{0:T(128)S(1)}, u32[]{:S(2)}, u32[]{:S(2)}) collective-permute-start(s32[64]{0:T(128)S(1)} %copy.49), channel_id=1, source_target_pairs={{8,0},{16,8},{24,16},{0,24},{9,1},{17,9},{25,17},{1,25},{10,2},{18... | collective-permute-start | bytes 776 | tf_op jit(solution)/shard_map/while/body/eval_jaxpr/ppermute | solution.py:23
  1016.4 164.6 %collective-permute-start = (bf16[64,128,128]{2,0,1:T(8,128)(2,1)S(1)}, bf16[64,128,128]{2,0,1:T(8,128)(2,1)}, u32[]{:S(2)}, u32[]{:S(2)}) collective-permute-start(bf16[64,128,128]{2,0,1:T(8,128)(2,1)S(1)} %copy.46), channel_id=1, source_target_pairs={{1,0},{2,1},{3,2},{4,3},{5,4},{6,5},{7,6},{0,7},{9,8},{10,9},{11,1... | collective-permute-start | bytes 6291464 | tf_op jit(solution)/shard_map/while/body/eval_jaxpr/ppermute | solution.py:23
  1016.4 164.5 %collective-permute-start.1 = (s32[64]{0:T(128)S(1)}, s32[64]{0:T(128)S(1)}, u32[]{:S(2)}, u32[]{:S(2)}) collective-permute-start(s32[64]{0:T(128)S(1)} %copy.47), channel_id=1, source_target_pairs={{1,0},{2,1},{3,2},{4,3},{5,4},{6,5},{7,6},{0,7},{9,8},{10,9},{11,1... | collective-permute-start | bytes 776 | tf_op jit(solution)/shard_map/while/body/eval_jaxpr/ppermute | solution.py:23
  1019.7 161.3 %collective-permute-start.2 = (bf16[64,128,128]{2,0,1:T(8,128)(2,1)}, bf16[64,128,128]{2,0,1:T(8,128)(2,1)}, u32[]{:S(2)}, u32[]{:S(2)}) collective-permute-start(bf16[64,128,128]{2,0,1:T(8,128)(2,1)} %copy.48), channel_id=1, source_target_pairs={{8,0},{16,8},{24,16},{0,24},{9,1},{17,9},{25,17},{1,25},{10,2},{18... | collective-permute-start | bytes 6291464 | tf_op jit(solution)/shard_map/while/body/eval_jaxpr/ppermute | solution.py:23
  1021.2 159.8 %collective-permute-start.3 = (s32[64]{0:T(128)S(1)}, s32[64]{0:T(128)S(1)}, u32[]{:S(2)}, u32[]{:S(2)}) collective-permute-start(s32[64]{0:T(128)S(1)} %copy.49), channel_id=1, source_target_pairs={{8,0},{16,8},{24,16},{0,24},{9,1},{17,9},{25,17},{1,25},{10,2},{18... | collective-permute-start | bytes 776 | tf_op jit(solution)/shard_map/while/body/eval_jaxpr/ppermute | solution.py:23
  1182.6 169.3 %collective-permute-start = (bf16[64,128,128]{2,0,1:T(8,128)(2,1)S(1)}, bf16[64,128,128]{2,0,1:T(8,128)(2,1)}, u32[]{:S(2)}, u32[]{:S(2)}) collective-permute-start(bf16[64,128,128]{2,0,1:T(8,128)(2,1)S(1)} %copy.46), channel_id=1, source_target_pairs={{1,0},{2,1},{3,2},{4,3},{5,4},{6,5},{7,6},{0,7},{9,8},{10,9},{11,1... | collective-permute-start | bytes 6291464 | tf_op jit(solution)/shard_map/while/body/eval_jaxpr/ppermute | solution.py:23
  1184.1 167.8 %collective-permute-start.1 = (s32[64]{0:T(128)S(1)}, s32[64]{0:T(128)S(1)}, u32[]{:S(2)}, u32[]{:S(2)}) collective-permute-start(s32[64]{0:T(128)S(1)} %copy.47), channel_id=1, source_target_pairs={{1,0},{2,1},{3,2},{4,3},{5,4},{6,5},{7,6},{0,7},{9,8},{10,9},{11,1... | collective-permute-start | bytes 776 | tf_op jit(solution)/shard_map/while/body/eval_jaxpr/ppermute | solution.py:23
  1189.5 162.4 %collective-permute-start.2 = (bf16[64,128,128]{2,0,1:T(8,128)(2,1)}, bf16[64,128,128]{2,0,1:T(8,128)(2,1)}, u32[]{:S(2)}, u32[]{:S(2)}) collective-permute-start(bf16[64,128,128]{2,0,1:T(8,128)(2,1)} %copy.48), channel_id=1, source_target_pairs={{8,0},{16,8},{24,16},{0,24},{9,1},{17,9},{25,17},{1,25},{10,2},{18... | collective-permute-start | bytes 6291464 | tf_op jit(solution)/shard_map/while/body/eval_jaxpr/ppermute | solution.py:23
  1192.1 159.8 %collective-permute-start.3 = (s32[64]{0:T(128)S(1)}, s32[64]{0:T(128)S(1)}, u32[]{:S(2)}, u32[]{:S(2)}) collective-permute-start(s32[64]{0:T(128)S(1)} %copy.49), channel_id=1, source_target_pairs={{8,0},{16,8},{24,16},{0,24},{9,1},{17,9},{25,17},{1,25},{10,2},{18... | collective-permute-start | bytes 776 | tf_op jit(solution)/shard_map/while/body/eval_jaxpr/ppermute | solution.py:23
  1353.5 164.4 %collective-permute-start = (bf16[64,128,128]{2,0,1:T(8,128)(2,1)S(1)}, bf16[64,128,128]{2,0,1:T(8,128)(2,1)}, u32[]{:S(2)}, u32[]{:S(2)}) collective-permute-start(bf16[64,128,128]{2,0,1:T(8,128)(2,1)S(1)} %copy.46), channel_id=1, source_target_pairs={{1,0},{2,1},{3,2},{4,3},{5,4},{6,5},{7,6},{0,7},{9,8},{10,9},{11,1... | collective-permute-start | bytes 6291464 | tf_op jit(solution)/shard_map/while/body/eval_jaxpr/ppermute | solution.py:23
  1353.5 164.4 %collective-permute-start.1 = (s32[64]{0:T(128)S(1)}, s32[64]{0:T(128)S(1)}, u32[]{:S(2)}, u32[]{:S(2)}) collective-permute-start(s32[64]{0:T(128)S(1)} %copy.47), channel_id=1, source_target_pairs={{1,0},{2,1},{3,2},{4,3},{5,4},{6,5},{7,6},{0,7},{9,8},{10,9},{11,1... | collective-permute-start | bytes 776 | tf_op jit(solution)/shard_map/while/body/eval_jaxpr/ppermute | solution.py:23
  1356.7 161.3 %collective-permute-start.2 = (bf16[64,128,128]{2,0,1:T(8,128)(2,1)}, bf16[64,128,128]{2,0,1:T(8,128)(2,1)}, u32[]{:S(2)}, u32[]{:S(2)}) collective-permute-start(bf16[64,128,128]{2,0,1:T(8,128)(2,1)} %copy.48), channel_id=1, source_target_pairs={{8,0},{16,8},{24,16},{0,24},{9,1},{17,9},{25,17},{1,25},{10,2},{18... | collective-permute-start | bytes 6291464 | tf_op jit(solution)/shard_map/while/body/eval_jaxpr/ppermute | solution.py:23
  1358.2 159.8 %collective-permute-start.3 = (s32[64]{0:T(128)S(1)}, s32[64]{0:T(128)S(1)}, u32[]{:S(2)}, u32[]{:S(2)}) collective-permute-start(s32[64]{0:T(128)S(1)} %copy.49), channel_id=1, source_target_pairs={{8,0},{16,8},{24,16},{0,24},{9,1},{17,9},{25,17},{1,25},{10,2},{18... | collective-permute-start | bytes 776 | tf_op jit(solution)/shard_map/while/body/eval_jaxpr/ppermute | solution.py:23
  1519.6 167.0 %collective-permute-start = (bf16[64,128,128]{2,0,1:T(8,128)(2,1)S(1)}, bf16[64,128,128]{2,0,1:T(8,128)(2,1)}, u32[]{:S(2)}, u32[]{:S(2)}) collective-permute-start(bf16[64,128,128]{2,0,1:T(8,128)(2,1)S(1)} %copy.46), channel_id=1, source_target_pairs={{1,0},{2,1},{3,2},{4,3},{5,4},{6,5},{7,6},{0,7},{9,8},{10,9},{11,1... | collective-permute-start | bytes 6291464 | tf_op jit(solution)/shard_map/while/body/eval_jaxpr/ppermute | solution.py:23
  1519.6 167.0 %collective-permute-start.1 = (s32[64]{0:T(128)S(1)}, s32[64]{0:T(128)S(1)}, u32[]{:S(2)}, u32[]{:S(2)}) collective-permute-start(s32[64]{0:T(128)S(1)} %copy.47), channel_id=1, source_target_pairs={{1,0},{2,1},{3,2},{4,3},{5,4},{6,5},{7,6},{0,7},{9,8},{10,9},{11,1... | collective-permute-start | bytes 776 | tf_op jit(solution)/shard_map/while/body/eval_jaxpr/ppermute | solution.py:23
  1524.1 162.5 %collective-permute-start.2 = (bf16[64,128,128]{2,0,1:T(8,128)(2,1)}, bf16[64,128,128]{2,0,1:T(8,128)(2,1)}, u32[]{:S(2)}, u32[]{:S(2)}) collective-permute-start(bf16[64,128,128]{2,0,1:T(8,128)(2,1)} %copy.48), channel_id=1, source_target_pairs={{8,0},{16,8},{24,16},{0,24},{9,1},{17,9},{25,17},{1,25},{10,2},{18... | collective-permute-start | bytes 6291464 | tf_op jit(solution)/shard_map/while/body/eval_jaxpr/ppermute | solution.py:23
  1526.8 159.9 %collective-permute-start.3 = (s32[64]{0:T(128)S(1)}, s32[64]{0:T(128)S(1)}, u32[]{:S(2)}, u32[]{:S(2)}) collective-permute-start(s32[64]{0:T(128)S(1)} %copy.49), channel_id=1, source_target_pairs={{8,0},{16,8},{24,16},{0,24},{9,1},{17,9},{25,17},{1,25},{10,2},{18... | collective-permute-start | bytes 776 | tf_op jit(solution)/shard_map/while/body/eval_jaxpr/ppermute | solution.py:23
  1702.7 47.5 %copy-start.4 = (s32[64]{0:T(128)S(1)}, s32[64]{0:T(128)}, u32[]{:S(2)}) copy-start(s32[64]{0:T(128)} %fusion.26) | copy-start | bytes 772
  1789.0 78.4 %copy-start.1 = (pred[64]{0:T(512)(128)(4,1)S(1)}, pred[64]{0:T(512)(128)(4,1)}, u32[]{:S(2)}) copy-start(pred[64]{0:T(512)(128)(4,1)} %iota_compare_fusion.4) | copy-start | bytes 196
Sparse Core Ops, SparseCore 0:
  21.1 353.9 all-reduce.1
where the time goes:
time: 1900 us; the launch traced here: 1880 us
  matrix products  902 us (47%)
  local copies, waits for them, and re-layouts  499 us (26%)
  waiting for transfers between devices  387 us (20%)
  starting transfers between devices  43.6 us (2%)
  other arithmetic  31.6 us (2%)
    dot_general x8, matrix products, step_product(): jnp.einsum('qak,kqb->qab', left_rows, right_cols, preferred_element_type=...  641 us
    reshape x7, local copies, waits for them, and re-layouts, step_product(): left_rows.astype(jnp.bfloat16).reshape(q_row.shape[0], 128, tile_cols * 128)  345 us
    psum x1, waiting for transfers between devices, from_root(): return lax.psum(block, axis)  330 us
    dot_general x8, matrix products, step_product(): jnp.einsum('skq,sab->kaqb', pick_right, s_blocks, preferred_element_type=...  124 us
    dot_general x8, matrix products, step_product(): jnp.einsum('pqk,pab->qakb', pick_left, p_blocks, preferred_element_type=j...  112 us
    ppermute x36, waiting for transfers between devices, shifted(): return lax.ppermute(block, axis, route)  56.8 us
    convert_element_type x1, local copies, waits for them, and re-layouts, step_product(): left_rows.astype(jnp.bfloat16).reshape(q_row.shape[0], 128, tile_cols * 128)  47.4 us
    ppermute x36, starting transfers between devices, shifted(): return lax.ppermute(block, axis, route)  43.6 us
  transfers between devices with their start and end apart: 37, of which 5 were waited for; matrix products, arithmetic and copies ran while one was open for 65% of the time, Pallas kernels for 0%

commit v1 on v0

v1 whole, which is shorter than its diff:
```python
import functools

import jax
import jax.numpy as jnp
from jax import lax
from jax.experimental import pallas as pl
from jax.experimental.pallas import tpu as pltpu
from jax.sharding import PartitionSpec as P

MESH = pl.DeviceIdType.MESH
MIB = 1 << 20


def rows_kernel(rows_n, cols_n, coeffs, out, send, recv):
    row, col = lax.axis_index("row"), lax.axis_index("col")
    sub = cols_n // rows_n
    height = out.shape[0]
    piece = height // rows_n
    half, share = lax.rem(col, sub), lax.div(col, sub)
    owner = lax.div(col, sub)
    targets = [
        {"row": lax.rem(row + step, rows_n), "col": row * sub + half} for step in range(1, rows_n)
    ]
    sources = [{"row": owner, "col": part * sub + half} for part in range(rows_n)]
    barrier = pltpu.get_barrier_semaphore()
    for device in targets:
        pl.semaphore_signal(barrier, inc=1, device_id=device, device_id_type=MESH)

    @pl.when(row != owner)
    def _():
        for device in sources:
            pl.semaphore_signal(barrier, inc=1, device_id=device, device_id_type=MESH)

    pl.semaphore_wait(barrier, rows_n - 1 + jnp.where(row != owner, rows_n, 0))

    def copy(step, part, device):
        start = half * height + share * piece
        return pltpu.make_async_remote_copy(
            src_ref=coeffs.at[pl.ds(pl.multiple_of(start, piece), piece)],
            dst_ref=out.at[pl.ds(pl.multiple_of(part * piece, piece), piece)],
            send_sem=send.at[step],
            recv_sem=recv.at[part],
            device_id=device,
            device_id_type=MESH,
        )

    sends = [copy(step, share, device) for step, device in enumerate(targets)]
    for one in sends:
        one.start()

    @pl.when(row != owner)
    def _():
        for part, device in enumerate(sources):
            copy(0, part, device).wait_recv()

    for one in sends:
        one.wait_send()


def gather_rows(coeffs, rows_n, cols_n):
    height = coeffs.shape[0] * rows_n // cols_n
    return pl.pallas_call(
        functools.partial(rows_kernel, rows_n, cols_n),
        out_shape=jax.ShapeDtypeStruct((height, coeffs.shape[1]), coeffs.dtype),
        in_specs=[pl.BlockSpec(memory_space=pl.ANY)],
        out_specs=pl.BlockSpec(memory_space=pl.ANY),
        scratch_shapes=[
            pltpu.SemaphoreType.DMA((rows_n - 1,)),
            pltpu.SemaphoreType.DMA((rows_n,)),
        ],
        compiler_params=pltpu.CompilerParams(collective_id=0, has_side_effects=True),
    )(coeffs)


def density_kernel(rows_n, cols_n, ids, count, coeffs, others, out, left, right, sem):
    row, col = lax.axis_index("row"), lax.axis_index("col")
    sub = cols_n // rows_n
    height = others.shape[0]
    tile_cols = height // 128
    load_left = pltpu.make_async_copy(coeffs, left, sem.at[0])
    load_left.start()
    here = row == lax.div(col, sub)
    start = pl.multiple_of(lax.rem(col, sub) * height, height)
    load_own = pltpu.make_async_copy(coeffs.at[pl.ds(start, height)], right, sem.at[1])
    load_other = pltpu.make_async_copy(others, right, sem.at[1])

    @pl.when(here)
    def _():
        load_own.start()

    @pl.when(jnp.logical_not(here))
    def _():
        load_other.start()

    live = count[0]
    load_left.wait()
    load_other.wait()

    def block(slot, carry):
        a = pl.multiple_of(lax.div(ids[slot], tile_cols) * 128, 128)
        b = pl.multiple_of(lax.rem(ids[slot], tile_cols) * 128, 128)
        raw = lax.dot_general(
            left[pl.ds(a, 128), :],
            right[pl.ds(b, 128), :],
            (((1,), (1,)), ((), ())),
            preferred_element_type=jnp.float32,
        )
        out[slot] = raw.astype(out.dtype)
        return carry

    def clear(slot, carry):
        out[slot] = jnp.zeros(out.shape[1:], out.dtype)
        return carry

    lax.fori_loop(0, live, block, 0)
    lax.fori_loop(live, out.shape[0], clear, 0)


def density(ids, count, coeffs, others, rows_n, cols_n):
    slots = ids.shape[0]
    return pl.pallas_call(
        functools.partial(density_kernel, rows_n, cols_n),
        out_shape=jax.ShapeDtypeStruct((slots, 128, 128), jnp.bfloat16),
        in_specs=[pl.BlockSpec(memory_space=pltpu.SMEM)] * 2
        + [pl.BlockSpec(memory_space=pl.ANY)] * 2,
        out_specs=pl.BlockSpec(memory_space=pltpu.VMEM),
        scratch_shapes=[
            pltpu.VMEM(coeffs.shape, coeffs.dtype),
            pltpu.VMEM(others.shape, coeffs.dtype),
            pltpu.SemaphoreType.DMA((2,)),
        ],
        compiler_params=pltpu.CompilerParams(vmem_limit_bytes=40 * MIB),
    )(ids, count, coeffs, others)


def blocks_kernel(rows_n, cols_n, parts, p_own, s_own, p_all, s_all, *sems):
    send, recv, pass_send, pass_recv, s_send, s_recv = sems
    row, col = lax.axis_index("row"), lax.axis_index("col")
    length = cols_n // 2
    z, core = lax.div(col, 2), lax.rem(col, 2)
    size = p_own.shape[0] // parts
    right, left = {"row": row, "col": col + 2}, {"row": row, "col": col - 2}
    partner = {"row": row, "col": z * 2 + 1 - core}
    column = [{"row": lax.rem(row + step, rows_n), "col": col} for step in range(1, rows_n)]
    has_right, has_left = z + 1 < length, z > 0

    barrier = pltpu.get_barrier_semaphore()

    def greet(device):
        pl.semaphore_signal(barrier, inc=1, device_id=device, device_id_type=MESH)

    greet(partner)
    for device in column:
        greet(device)

    @pl.when(has_right)
    def _():
        greet(right)

    @pl.when(has_left)
    def _():
        greet(left)

    pl.semaphore_wait(barrier, rows_n + jnp.where(has_right, 1, 0) + jnp.where(has_left, 1, 0))

    def remote(src, dst, send_sem, recv_sem, device):
        return pltpu.make_async_remote_copy(
            src_ref=src,
            dst_ref=dst,
            send_sem=send_sem,
            recv_sem=recv_sem,
            device_id=device,
            device_id_type=MESH,
        )

    def piece(source, lane, part):
        return p_all.at[source * 2 + lane, pl.ds(part * size, size)]

    def origin(way, step):
        return z - step if way == 0 else z + step

    def sent(way, step, part):
        where = piece(origin(way, step), core, part)
        src = p_own.at[pl.ds(part * size, size)] if step == 0 else where
        device = right if way == 0 else left
        return remote(src, where, send.at[way, step, part], recv.at[way, step, part], device)

    def passed(way, step, part):
        where = piece(origin(way, step), core, part)
        src = p_own.at[pl.ds(part * size, size)] if step == 0 else where
        return remote(
            src, where, pass_send.at[way, step, part], pass_recv.at[way, step, part], partner
        )

    def onward(way):
        return has_right if way == 0 else has_left

    def exists(way, step):
        return z >= step if way == 0 else z + step < length

    for part in range(parts):
        for way in range(2):
            pl.when(onward(way))(lambda way=way: sent(way, 0, part).start())
    s_sends = [
        remote(s_own, s_all.at[row], s_send.at[n], s_recv.at[n], device)
        for n, device in enumerate(column)
    ]
    for one in s_sends:
        one.start()
    for part in range(parts):
        passed(0, 0, part).start()
    for step in range(1, length):
        for part in range(parts):
            for way in range(2):

                @pl.when(exists(way, step))
                def _():
                    sent(way, step - 1, part).wait_recv()
                    passed(way, step, part).start()
                    if step < length - 1:
                        pl.when(onward(way))(lambda: sent(way, step, part).start())

    for part in range(parts):
        passed(0, 0, part).wait()
        for way in range(2):
            pl.when(onward(way))(lambda way=way: sent(way, 0, part).wait_send())
    for step in range(1, length):
        for part in range(parts):
            for way in range(2):

                @pl.when(exists(way, step))
                def _():
                    passed(way, step, part).wait()
                    if step < length - 1:
                        pl.when(onward(way))(lambda: sent(way, step, part).wait_send())

    for one in s_sends:
        one.wait()


def gather_blocks(p_own, s_own, rows_n, cols_n):
    parts = 4 if p_own.shape[0] % 4 == 0 else 1
    table = pltpu.SemaphoreType.DMA((2, cols_n // 2, parts))
    return pl.pallas_call(
        functools.partial(blocks_kernel, rows_n, cols_n, parts),
        out_shape=(
            jax.ShapeDtypeStruct((cols_n,) + p_own.shape, p_own.dtype),
            jax.ShapeDtypeStruct((rows_n,) + s_own.shape, s_own.dtype),
        ),
        in_specs=[pl.BlockSpec(memory_space=pl.ANY)] * 2,
        out_specs=[pl.BlockSpec(memory_space=pl.ANY)] * 2,
        scratch_shapes=[table] * 4 + [pltpu.SemaphoreType.DMA((rows_n - 1,))] * 2,
        compiler_params=pltpu.CompilerParams(collective_id=1, has_side_effects=True),
    )(p_own, s_own)


def product_kernel(rows_n, cols_n, codes, counts, p_own, s_own, p_all, s_all, out, left, right, sem):
    row, col = lax.axis_index("row"), lax.axis_index("col")
    p_max, s_max = p_own.shape[0], s_own.shape[0]
    base = rows_n * s_max
    loads = [pltpu.make_async_copy(p_own, left.at[pl.ds(col * p_max, p_max)], sem.at[0])]
    loads += [pltpu.make_async_copy(s_own, right.at[pl.ds(row * s_max, s_max)], sem.at[1])]
    for step in range(1, cols_n):
        at = lax.rem(col + step, cols_n)
        loads += [
            pltpu.make_async_copy(
                p_all.at[at], left.at[pl.ds(at * p_max, p_max)], sem.at[len(loads)]
            )
        ]
    for step in range(1, rows_n):
        at = lax.rem(row + step, rows_n)
        loads += [
            pltpu.make_async_copy(
                s_all.at[at], right.at[pl.ds(at * s_max, s_max)], sem.at[len(loads)]
            )
        ]
    for load in loads:
        load.start()
    for load in loads:
        load.wait()

    def slot(q, carry):
        def term(n, total):
            code = codes[q, n]
            return total + jnp.dot(
                left[lax.div(code, base)],
                right[lax.rem(code, base)],
                preferred_element_type=jnp.float32,
            )

        out[q] = lax.fori_loop(0, counts[q], term, jnp.zeros((128, 128), jnp.float32))
        return carry

    lax.fori_loop(0, out.shape[0], slot, 0)


def block_product(codes, counts, p_own, s_own, p_all, s_all):
    cols_n, p_max = p_all.shape[:2]
    rows_n, s_max = s_all.shape[:2]
    return pl.pallas_call(
        functools.partial(product_kernel, rows_n, cols_n),
        out_shape=jax.ShapeDtypeStruct((counts.shape[0], 128, 128), jnp.float32),
        in_specs=[pl.BlockSpec(memory_space=pltpu.SMEM)] * 2
        + [pl.BlockSpec(memory_space=pl.ANY)] * 4,
        out_specs=pl.BlockSpec(memory_space=pltpu.VMEM),
        scratch_shapes=[
            pltpu.VMEM((cols_n * p_max, 128, 128), p_all.dtype),
            pltpu.VMEM((rows_n * s_max, 128, 128), s_all.dtype),
            pltpu.SemaphoreType.DMA((cols_n + rows_n,)),
        ],
        compiler_params=pltpu.CompilerParams(vmem_limit_bytes=40 * MIB),
    )(codes, counts, p_own, s_own, p_all, s_all)


def match_lists(p_codes, s_codes, q_ids, q_live, tile_cols, span):
    cols_n, p_max = p_codes.shape
    rows_n, s_max = s_codes.shape
    q_row, q_col = q_ids // tile_cols, q_ids % tile_cols
    at = jnp.arange(tile_cols, dtype=jnp.int32)
    p_want = q_row[:, None] * tile_cols + at[None, :]
    p_hit = p_codes[None, :, None, :] == p_want[:, None, :, None]
    p_slot = jnp.arange(cols_n * p_max, dtype=jnp.int32).reshape(1, cols_n, 1, p_max)
    p_at = jnp.max(jnp.where(p_hit, p_slot, -1), axis=3)
    level = jnp.arange(span * tile_cols, dtype=jnp.int32).reshape(span, tile_cols)
    s_want = level[None] * tile_cols + q_col[:, None, None]
    s_hit = s_codes[None, None, :, None, :] == s_want[:, :, None, :, None]
    s_slot = jnp.arange(rows_n * s_max, dtype=jnp.int32).reshape(1, 1, rows_n, 1, s_max)
    s_at = jnp.max(jnp.where(s_hit, s_slot, -1), axis=4)
    p_at = p_at.reshape(q_ids.shape[0], -1)
    s_at = s_at.reshape(q_ids.shape[0], -1)
    depth = p_at.shape[1]
    match = (p_at >= 0) & (s_at >= 0) & q_live[:, None]
    code = jnp.where(match, p_at * (rows_n * s_max) + s_at, 0)
    order = jnp.arange(depth, dtype=jnp.int32)
    before = order[None, :, None] > order[None, None, :]
    rank = jnp.sum((before & match[:, None, :]).astype(jnp.int32), axis=2)
    rank = jnp.where(match, rank, -1)
    picked = rank[:, None, :] == order[None, :, None]
    codes = jnp.sum(jnp.where(picked, code[:, None, :], 0), axis=2)
    return codes, jnp.sum(match.astype(jnp.int32), axis=1)


def on_device(coeffs, p_slots, p_count, s_blocks, s_slots, s_count, q_slots, q_count):
    rows_n = lax.axis_size("row")
    cols_n = lax.axis_size("col")
    tile_cols = coeffs.shape[0] * rows_n // cols_n // 128
    p_ids, s_ids, q_ids = p_slots[0, 0], s_slots[0, 0], q_slots[0, 0]
    s_own = s_blocks[0, 0]
    p_max, s_max, q_max = p_ids.shape[0], s_ids.shape[0], q_ids.shape[0]

    def live(ids, count):
        return jnp.arange(ids.shape[0], dtype=jnp.int32) < count[0, 0]

    p_codes = lax.all_gather(jnp.where(live(p_ids, p_count), p_ids, -1), "col")
    s_codes = lax.all_gather(jnp.where(live(s_ids, s_count), s_ids, -1), "row")
    codes, counts = match_lists(
        p_codes, s_codes, q_ids, live(q_ids, q_count), tile_cols, cols_n // rows_n
    )
    others = gather_rows(coeffs, rows_n, cols_n)
    p_own = density(p_ids, p_count[0], coeffs, others, rows_n, cols_n)
    p_all, s_all = gather_blocks(p_own, s_own, rows_n, cols_n)
    product = block_product(codes, counts, p_own, s_own, p_all, s_all)
    return (p_own.reshape(1, 1, p_max, 128, 128), product.reshape(1, 1, q_max, 128, 128))


def solution(mesh):
    return jax.shard_map(
        on_device,
        mesh=mesh,
        in_specs=(
            P("row", None),
            P("row", "col", None),
            P("row", "col"),
            P("row", "col", None, None, None),
            P("row", "col", None),
            P("row", "col"),
            P("row", "col", None),
            P("row", "col"),
        ),
        out_specs=(P("row", "col", None, None, None), P("row", "col", None, None, None)),
        check_vma=False,
    )
```

time: 1900 us -> 644 us (0.34)
  matrix products: 902 us -> 0 us
  Pallas kernels: 0 us -> 583 us
  local copies, waits for them, and re-layouts: 499 us -> 8.99 us
  waiting for transfers between devices: 387 us -> 0 us
  starting transfers between devices: 43.6 us -> 0 us
  blocking collectives: 0 us -> 21.4 us
    dot_general x25 -> x0, matrix products: 902 us -> none  [the longest x8 641 us: step_product(): jnp.einsum('qak,kqb->qab', left_rows, right_cols, preferred_element_type=...]
    pallas_call x0 -> x4, Pallas kernels: none -> 583 us  [the longest x1 327 us: gather_blocks(): pl.pallas_call(functools.partial(blocks_kernel, rows_n, cols_n, parts), o...]
    reshape x7 -> x1, local copies, waits for them, and re-layouts: 345 us -> 0.08 us  [match_lists(): s_at = s_at.reshape(q_ids.shape[0], -1)]
    psum x1 -> x0, waiting for transfers between devices: 330 us -> none  [from_root(): return lax.psum(block, axis)]
    convert_element_type x2 -> x0, local copies, waits for them, and re-layouts: 70.6 us -> none  [the longest x1 47.4 us: step_product(): left_rows.astype(jnp.bfloat16).reshape(q_row.shape[0], 128, tile_cols * 128)]
    ppermute x36 -> x0, waiting for transfers between devices: 56.8 us -> none  [shifted(): return lax.ppermute(block, axis, route)]
    ppermute x36 -> x0, starting transfers between devices: 43.6 us -> none  [shifted(): return lax.ppermute(block, axis, route)]
    gather x2 -> x0, local copies, waits for them, and re-layouts: 35.1 us -> none  [the longest x1 19.3 us: on_device(): left = coeffs.reshape(tile_rows, 128, orbitals)[slot_ids // tile_cols]]
  transfers between devices with their start and end apart: 37 -> 0, of which waited for: 5 -> 0; matrix products, arithmetic and copies ran while one was open for 65% -> 0% of each run, Pallas kernels for 0% -> 0%
where the time goes in v1:
time: 644 us; the launch traced here: 641 us
  Pallas kernels  583 us (91%)
  other arithmetic  25 us (4%)
  blocking collectives  21.4 us (3%)
  local copies, waits for them, and re-layouts  8.99 us (1%)
    pallas_call x1, Pallas kernels, gather_blocks(): pl.pallas_call(functools.partial(blocks_kernel, rows_n, cols_n, parts), o...  327 us
    pallas_call x1, Pallas kernels, gather_rows(): pl.pallas_call(functools.partial(rows_kernel, rows_n, cols_n), out_shape=...  228 us
    pallas_call x1, Pallas kernels, density(): pl.pallas_call(functools.partial(density_kernel, rows_n, cols_n), out_sha...  16.7 us

profile of v1, /device:TPU:0, one launch (start us, length us, event | category | flops | bytes accessed | tf_op | source)
XLA Modules:
  0.0 641.1 jit_solution(8875639585233294985)
XLA Ops:
  2.6 0.7 fusion.1
  3.2 0.7 fusion
  3.9 0.7 and_select_fusion
  4.6 9.4 %all-gather.1 = s32[4,1,64]{2,1,0:T(1,128)S(1)} all-gather(s32[1,1,64]{2,1,0:T(1,128)S(1)} %fusion.1), channel_id=1, replica_groups=mesh['row'=4,'col'=8] {'row'}, dimensions={0}, use_global_device_ids=true | all-gather | bytes 1280 | tf_op jit(solution)/shard_map/all_gather | solution.py:355
  14.0 12.0 %all-gather = s32[8,1,64]{2,1,0:T(1,128)S(1)} all-gather(s32[1,1,64]{2,1,0:T(1,128)S(1)} %fusion), channel_id=1, replica_groups=mesh['row'=4,'col'=8] {'col'}, dimensions={0}, use_global_device_ids=true | all-gather | bytes 2304 | tf_op jit(solution)/shard_map/all_gather | solution.py:354
  26.0 0.1 iota_add_fusion
  26.1 0.1 broadcast_add_fusion
  26.2 9.4 %select_reduce_fusion.1 = s32[64,2,4,16]{3,2,1,0:T(4,128)S(1)} fusion(s32[4,64]{1,0:T(4,128)S(1)} %multiply_add_fusion.1, s32[64,2,16]{2,1,0:T(2,128)S(1)} %broadcast_add_fusion, s32[4,64]{1,0:T(4,128)S(1)} %bitcast.53), kind=kLoop, calls=%fused_computation.3 | loop fusion | flops 1564672 | bytes 43008 | tf_op jit(solution)/shard_map/reduce_max | solution.py:328
  35.6 0.1 copy.24
  35.7 0.1 copy.25
  35.8 8.9 %select_reduce_fusion.2 = s32[64,8,16]{2,1,0:T(8,128)S(1)} fusion(s32[8,64]{1,0:T(8,128)S(1)} %multiply_add_fusion, s32[64,16]{1,0:T(8,128)S(1)} %iota_add_fusion, s32[8,64]{1,0:T(8,128)S(1)} %bitcast.52), kind=kLoop, calls=%fused_computation.4 | loop fusion | flops 1564672 | bytes 40960 | tf_op jit(solution)/shard_map/reduce_max | solution.py:323
  44.7 0.1 copy.27
  44.8 0.1 copy.28
  44.9 1.3 convert_reduce_fusion.1.counts
  46.3 0.1 copy.23
  46.4 0.1 copy.26
  46.5 0.1 add_select_fusion
  46.6 1.4 convert_reduce_fusion
  48.0 1.7 select_reduce_fusion.codes
  49.7 0.0 copy-start.4
  49.7 228.1 %shard_map.95.others = bf16[2048,2048]{1,0:T(8,128)(2,1)} custom-call(bf16[4096,2048]{1,0:T(8,128)(2,1)} %coeffs.3), custom_call_target="tpu_custom_call" | custom-call | tf_op jit(solution)/shard_map/pallas_call | solution.py:62
  277.8 0.0 copy-done.4
  277.8 0.0 copy-start
  277.8 3.4 copy-done
  281.2 16.7 %shard_map.96.p_own = bf16[64,128,128]{2,1,0:T(8,128)(2,1)} custom-call(s32[64]{0:T(128)S(1)} %bitcast.46, s32[1]{0:T(128)} %bitcast.39.count, bf16[4096,2048]{1,0:T(8,128)(2,1)} %coeffs.3, bf16[2048,2048]{1,0:T(8,128)(2,1)S(1)} %copy-done), custom_call_target="tpu_custom_call" | custom-call | tf_op jit(solution)/shard_map/pallas_call | solution.py:121
  297.9 0.0 copy-start.1
  297.9 326.5 %shard_map.97 = (bf16[8,64,128,128]{3,2,1,0:T(8,128)(2,1)}, bf16[4,64,128,128]{3,2,1,0:T(8,128)(2,1)}) custom-call(bf16[64,128,128]{2,1,0:T(8,128)(2,1)} %shard_map.96.p_own, bf16[64,128,128]{2,1,0:T(8,128)(2,1)} %bitcast.44), custom_call_target="tpu_custom_call" | custom-call | tf_op jit(solution)/shard_map/pallas_call | solution.py:244
  624.4 0.0 copy-done.1
  624.4 0.0 copy-start.2
  624.4 3.4 copy-done.2
  627.8 0.0 copy-start.3
  627.8 1.6 copy-done.3
  629.4 11.5 %shard_map.98 = f32[64,128,128]{2,1,0:T(8,128)} custom-call(s32[64,128]{1,0:T(8,128)S(1)} %select_reduce_fusion.codes, s32[64]{0:T(128)S(1)} %convert_reduce_fusion.1.counts, bf16[64,128,128]{2,1,0:T(8,128)(2,1)S(1)} %copy-done.1, bf16[64,128,128]{2,1,0:T(8,128)(2,1)S(1)} %bitcast.45, bf16[8,64,128,128]{3,2,1,0:T(8,128)(2,1)} %get-tuple-element.4.p_all, ...), custom_call_target="tpu_custom_call" | custom-call | tf_op jit(solution)/shard_map/pallas_call | solution.py:300
  (8 shorter events, 0.1 us)
Async XLA Ops:
  49.7 228.1 %copy-start.4 = (s32[1,1,64]{2,1,0:T(1,128)S(1)}, s32[1,1,64]{2,1,0:T(1,128)}, u32[]{:S(2)}) copy-start(s32[1,1,64]{2,1,0:T(1,128)} %param.9) | copy-start | bytes 772
  277.8 3.4 copy-start
  297.9 326.6 %copy-start.1 = (bf16[64,128,128]{2,1,0:T(8,128)(2,1)S(1)}, bf16[64,128,128]{2,1,0:T(8,128)(2,1)}, u32[]{:S(2)}) copy-start(bf16[64,128,128]{2,1,0:T(8,128)(2,1)} %shard_map.96.p_own) | copy-start | bytes 6291460
  624.4 3.4 copy-start.2
  627.8 1.6 copy-start.3

commit v2 on v1

--- a/solution.py
+++ b/solution.py
@@ -57,17 +57,80 @@
         one.wait_send()
 
 
+def square_kernel(rows_n, cols_n, parts, coeffs, out, send, recv):
+    row, col = lax.axis_index("row"), lax.axis_index("col")
+    sub = cols_n // rows_n
+    height = out.shape[0]
+    size = height // (2 * parts)
+    owner = lax.div(col, sub)
+    first = lax.rem(col, sub) * height
+    y, x = lax.div(row, 2), lax.rem(row, 2)
+    dy = lax.rem(y + lax.div(owner, 2), 2)
+    dx = lax.rem(x + lax.rem(owner, 2), 2)
+    along_x, along_y = y * 2 + 1 - x, (1 - y) * 2 + x
+    is_source = row == owner
+    sends = [jnp.logical_or(dx == 1, dy == 0), jnp.logical_or(dx == 0, dy == 1)]
+    following = [
+        jnp.where(dx == dy, along_x, along_y),
+        jnp.where(dx == dy, along_y, along_x),
+    ]
+
+    barrier = pltpu.get_barrier_semaphore()
+    for near in (along_x, along_y):
+        pl.semaphore_signal(
+            barrier, inc=1, device_id={"row": near, "col": col}, device_id_type=MESH
+        )
+    pl.semaphore_wait(barrier, 2)
+
+    def copy(way, part, from_input):
+        offset = (way * parts + part) * size
+        where = out.at[pl.ds(offset, size)]
+        start = pl.multiple_of(first + offset, size)
+        return pltpu.make_async_remote_copy(
+            src_ref=coeffs.at[pl.ds(start, size)] if from_input else where,
+            dst_ref=where,
+            send_sem=send.at[way, part],
+            recv_sem=recv.at[way, part],
+            device_id={"row": following[way], "col": col},
+            device_id_type=MESH,
+        )
+
+    @pl.when(is_source)
+    def _():
+        for part in range(parts):
+            for way in range(2):
+                copy(way, part, True).start()
+
+    @pl.when(jnp.logical_not(is_source))
+    def _():
+        for part in range(parts):
+            for way in range(2):
+                copy(way, part, False).wait_recv()
+                pl.when(sends[way])(lambda: copy(way, part, False).start())
+
+    for way in range(2):
+
+        @pl.when(sends[way])
+        def _():
+            for part in range(parts):
+                copy(way, part, False).wait_send()
+
+
 def gather_rows(coeffs, rows_n, cols_n):
     height = coeffs.shape[0] * rows_n // cols_n
+    if rows_n == 4:
+        parts = max(1, height // 256)
+        body = functools.partial(square_kernel, rows_n, cols_n, parts)
+        sems = [pltpu.SemaphoreType.DMA((2, parts))] * 2
+    else:
+        body = functools.partial(rows_kernel, rows_n, cols_n)
+        sems = [pltpu.SemaphoreType.DMA((rows_n - 1,)), pltpu.SemaphoreType.DMA((rows_n,))]
     return pl.pallas_call(
-        functools.partial(rows_kernel, rows_n, cols_n),
+        body,
         out_shape=jax.ShapeDtypeStruct((height, coeffs.shape[1]), coeffs.dtype),
         in_specs=[pl.BlockSpec(memory_space=pl.ANY)],
         out_specs=pl.BlockSpec(memory_space=pl.ANY),
-        scratch_shapes=[
-            pltpu.SemaphoreType.DMA((rows_n - 1,)),
-            pltpu.SemaphoreType.DMA((rows_n,)),
-        ],
+        scratch_shapes=sems,
         compiler_params=pltpu.CompilerParams(collective_id=0, has_side_effects=True),
     )(coeffs)
 

time: 644 us -> 532 us (0.83)
  Pallas kernels: 583 us -> 469 us
    pallas_call x1, Pallas kernels: 228 us -> 92.5 us  [gather_rows(): pl.pallas_call(body, out_shape=jax.ShapeDtypeStruct((height, coeffs.shape...]
    pallas_call x1, Pallas kernels: 327 us -> 343 us  [gather_blocks(): pl.pallas_call(functools.partial(blocks_kernel, rows_n, cols_n, parts), o...]
where the time goes in v2:
time: 532 us; the launch traced here: 528 us
  Pallas kernels  469 us (88%)
  other arithmetic  25 us (5%)
  blocking collectives  21.4 us (4%)
  local copies, waits for them, and re-layouts  8.99 us (2%)
    pallas_call x1, Pallas kernels, gather_blocks(): pl.pallas_call(functools.partial(blocks_kernel, rows_n, cols_n, parts), o...  343 us
    pallas_call x1, Pallas kernels, gather_rows(): pl.pallas_call(body, out_shape=jax.ShapeDtypeStruct((height, coeffs.shape...  92.5 us
    pallas_call x1, Pallas kernels, density(): pl.pallas_call(functools.partial(density_kernel, rows_n, cols_n), out_sha...  19.1 us
    pallas_call x1, Pallas kernels, block_product(): pl.pallas_call(functools.partial(product_kernel, rows_n, cols_n), out_sha...  14.5 us
    all_gather x1, blocking collectives, on_device(): p_codes = lax.all_gather(jnp.where(live(p_ids, p_count), p_ids, -1), 'col')  12 us

profile of v2, /device:TPU:0, one launch (start us, length us, event | category | flops | bytes accessed | tf_op | source)
XLA Modules:
  0.0 527.7 jit_solution(1789970472036976143)
XLA Ops:
  2.6 0.7 fusion.1
  3.2 0.7 fusion
  3.9 0.7 and_select_fusion
  4.6 9.4 %all-gather.1 = s32[4,1,64]{2,1,0:T(1,128)S(1)} all-gather(s32[1,1,64]{2,1,0:T(1,128)S(1)} %fusion.1), channel_id=1, replica_groups=mesh['row'=4,'col'=8] {'row'}, dimensions={0}, use_global_device_ids=true | all-gather | bytes 1280 | tf_op jit(solution)/shard_map/all_gather | solution.py:418
  14.0 12.0 %all-gather = s32[8,1,64]{2,1,0:T(1,128)S(1)} all-gather(s32[1,1,64]{2,1,0:T(1,128)S(1)} %fusion), channel_id=1, replica_groups=mesh['row'=4,'col'=8] {'col'}, dimensions={0}, use_global_device_ids=true | all-gather | bytes 2304 | tf_op jit(solution)/shard_map/all_gather | solution.py:417
  26.0 0.1 iota_add_fusion
  26.1 0.1 broadcast_add_fusion
  26.2 9.4 %select_reduce_fusion.1 = s32[64,2,4,16]{3,2,1,0:T(4,128)S(1)} fusion(s32[4,64]{1,0:T(4,128)S(1)} %multiply_add_fusion.1, s32[64,2,16]{2,1,0:T(2,128)S(1)} %broadcast_add_fusion, s32[4,64]{1,0:T(4,128)S(1)} %bitcast.53), kind=kLoop, calls=%fused_computation.3 | loop fusion | flops 1564672 | bytes 43008 | tf_op jit(solution)/shard_map/reduce_max | solution.py:391
  35.6 0.1 copy.24
  35.7 0.1 copy.25
  35.8 8.9 %select_reduce_fusion.2 = s32[64,8,16]{2,1,0:T(8,128)S(1)} fusion(s32[8,64]{1,0:T(8,128)S(1)} %multiply_add_fusion, s32[64,16]{1,0:T(8,128)S(1)} %iota_add_fusion, s32[8,64]{1,0:T(8,128)S(1)} %bitcast.52), kind=kLoop, calls=%fused_computation.4 | loop fusion | flops 1564672 | bytes 40960 | tf_op jit(solution)/shard_map/reduce_max | solution.py:386
  44.7 0.1 copy.27
  44.8 0.1 copy.28
  44.9 1.3 convert_reduce_fusion.1.counts
  46.3 0.1 copy.23
  46.4 0.1 copy.26
  46.5 0.1 add_select_fusion
  46.6 1.4 convert_reduce_fusion
  48.0 1.7 select_reduce_fusion.codes
  49.7 0.0 copy-start.4
  49.7 92.5 %shard_map.95.others = bf16[2048,2048]{1,0:T(8,128)(2,1)} custom-call(bf16[4096,2048]{1,0:T(8,128)(2,1)} %coeffs.3), custom_call_target="tpu_custom_call" | custom-call | tf_op jit(solution)/shard_map/pallas_call | solution.py:128
  142.2 0.0 copy-done.4
  142.2 0.0 copy-start
  142.2 3.4 copy-done
  145.6 19.1 %shard_map.96.p_own = bf16[64,128,128]{2,1,0:T(8,128)(2,1)} custom-call(s32[64]{0:T(128)S(1)} %bitcast.46, s32[1]{0:T(128)} %bitcast.39.count, bf16[4096,2048]{1,0:T(8,128)(2,1)} %coeffs.3, bf16[2048,2048]{1,0:T(8,128)(2,1)S(1)} %copy-done), custom_call_target="tpu_custom_call" | custom-call | tf_op jit(solution)/shard_map/pallas_call | solution.py:184
  164.7 0.0 copy-start.1
  164.7 343.3 %shard_map.97 = (bf16[8,64,128,128]{3,2,1,0:T(8,128)(2,1)}, bf16[4,64,128,128]{3,2,1,0:T(8,128)(2,1)}) custom-call(bf16[64,128,128]{2,1,0:T(8,128)(2,1)} %shard_map.96.p_own, bf16[64,128,128]{2,1,0:T(8,128)(2,1)} %bitcast.44), custom_call_target="tpu_custom_call" | custom-call | tf_op jit(solution)/shard_map/pallas_call | solution.py:307
  508.0 0.0 copy-done.1
  508.0 0.0 copy-start.2
  508.0 3.4 copy-done.2
  511.4 0.0 copy-start.3
  511.4 1.6 copy-done.3
  513.0 14.5 %shard_map.98 = f32[64,128,128]{2,1,0:T(8,128)} custom-call(s32[64,128]{1,0:T(8,128)S(1)} %select_reduce_fusion.codes, s32[64]{0:T(128)S(1)} %convert_reduce_fusion.1.counts, bf16[64,128,128]{2,1,0:T(8,128)(2,1)S(1)} %copy-done.1, bf16[64,128,128]{2,1,0:T(8,128)(2,1)S(1)} %bitcast.45, bf16[8,64,128,128]{3,2,1,0:T(8,128)(2,1)} %get-tuple-element.4.p_all, ...), custom_call_target="tpu_custom_call" | custom-call | tf_op jit(solution)/shard_map/pallas_call | solution.py:363
  (8 shorter events, 0.1 us)
Async XLA Ops:
  49.7 92.5 %copy-start.4 = (s32[1,1,64]{2,1,0:T(1,128)S(1)}, s32[1,1,64]{2,1,0:T(1,128)}, u32[]{:S(2)}) copy-start(s32[1,1,64]{2,1,0:T(1,128)} %param.9) | copy-start | bytes 772
  142.2 3.4 copy-start
  164.7 343.3 %copy-start.1 = (bf16[64,128,128]{2,1,0:T(8,128)(2,1)S(1)}, bf16[64,128,128]{2,1,0:T(8,128)(2,1)}, u32[]{:S(2)}) copy-start(bf16[64,128,128]{2,1,0:T(8,128)(2,1)} %shard_map.96.p_own) | copy-start | bytes 6291460
  508.0 3.4 copy-start.2
  511.4 1.6 copy-start.3

commit v3 on v2

--- a/solution.py
+++ b/solution.py
@@ -99,7 +99,12 @@
     def _():
         for part in range(parts):
             for way in range(2):
+                if part >= 2:
+                    copy(way, part - 2, True).wait_send()
                 copy(way, part, True).start()
+        for part in range(max(0, parts - 2), parts):
+            for way in range(2):
+                copy(way, part, True).wait_send()
 
     @pl.when(jnp.logical_not(is_source))
     def _():
@@ -110,7 +115,7 @@
 
     for way in range(2):
 
-        @pl.when(sends[way])
+        @pl.when(jnp.logical_and(sends[way], jnp.logical_not(is_source)))
         def _():
             for part in range(parts):
                 copy(way, part, False).wait_send()

time: 532 us -> 534 us (level); the launches traced: 528 us -> 524 us
  no operation moved by 1% of the time
where the time goes in v3:
time: 534 us; the launch traced here: 524 us
  Pallas kernels  465 us (87%)
  other arithmetic  25 us (5%)
  blocking collectives  21.4 us (4%)
  local copies, waits for them, and re-layouts  8.99 us (2%)
    pallas_call x1, Pallas kernels, gather_blocks(): pl.pallas_call(functools.partial(blocks_kernel, rows_n, cols_n, parts), o...  346 us
    pallas_call x1, Pallas kernels, gather_rows(): pl.pallas_call(body, out_shape=jax.ShapeDtypeStruct((height, coeffs.shape...  92.5 us
    pallas_call x1, Pallas kernels, density(): pl.pallas_call(functools.partial(density_kernel, rows_n, cols_n), out_sha...  14.3 us
    pallas_call x1, Pallas kernels, block_product(): pl.pallas_call(functools.partial(product_kernel, rows_n, cols_n), out_sha...  12.6 us
    all_gather x1, blocking collectives, on_device(): p_codes = lax.all_gather(jnp.where(live(p_ids, p_count), p_ids, -1), 'col')  12 us

profile of v3, /device:TPU:0, one launch (start us, length us, event | category | flops | bytes accessed | tf_op | source)
XLA Modules:
  0.0 523.6 jit_solution(14885874771019560093)
XLA Ops:
  2.6 0.7 fusion.1
  3.2 0.7 fusion
  3.9 0.7 and_select_fusion
  4.6 9.4 %all-gather.1 = s32[4,1,64]{2,1,0:T(1,128)S(1)} all-gather(s32[1,1,64]{2,1,0:T(1,128)S(1)} %fusion.1), channel_id=1, replica_groups=mesh['row'=4,'col'=8] {'row'}, dimensions={0}, use_global_device_ids=true | all-gather | bytes 1280 | tf_op jit(solution)/shard_map/all_gather | solution.py:423
  14.0 12.0 %all-gather = s32[8,1,64]{2,1,0:T(1,128)S(1)} all-gather(s32[1,1,64]{2,1,0:T(1,128)S(1)} %fusion), channel_id=1, replica_groups=mesh['row'=4,'col'=8] {'col'}, dimensions={0}, use_global_device_ids=true | all-gather | bytes 2304 | tf_op jit(solution)/shard_map/all_gather | solution.py:422
  26.0 0.1 iota_add_fusion
  26.1 0.1 broadcast_add_fusion
  26.2 9.4 %select_reduce_fusion.1 = s32[64,2,4,16]{3,2,1,0:T(4,128)S(1)} fusion(s32[4,64]{1,0:T(4,128)S(1)} %multiply_add_fusion.1, s32[64,2,16]{2,1,0:T(2,128)S(1)} %broadcast_add_fusion, s32[4,64]{1,0:T(4,128)S(1)} %bitcast.53), kind=kLoop, calls=%fused_computation.3 | loop fusion | flops 1564672 | bytes 43008 | tf_op jit(solution)/shard_map/reduce_max | solution.py:396
  35.6 0.1 copy.24
  35.7 0.1 copy.25
  35.8 8.9 %select_reduce_fusion.2 = s32[64,8,16]{2,1,0:T(8,128)S(1)} fusion(s32[8,64]{1,0:T(8,128)S(1)} %multiply_add_fusion, s32[64,16]{1,0:T(8,128)S(1)} %iota_add_fusion, s32[8,64]{1,0:T(8,128)S(1)} %bitcast.52), kind=kLoop, calls=%fused_computation.4 | loop fusion | flops 1564672 | bytes 40960 | tf_op jit(solution)/shard_map/reduce_max | solution.py:391
  44.7 0.1 copy.27
  44.8 0.1 copy.28
  44.9 1.3 convert_reduce_fusion.1.counts
  46.3 0.1 copy.23
  46.4 0.1 copy.26
  46.5 0.1 add_select_fusion
  46.6 1.4 convert_reduce_fusion
  48.0 1.7 select_reduce_fusion.codes
  49.7 0.0 copy-start.4
  49.7 92.5 %shard_map.95.others = bf16[2048,2048]{1,0:T(8,128)(2,1)} custom-call(bf16[4096,2048]{1,0:T(8,128)(2,1)} %coeffs.3), custom_call_target="tpu_custom_call" | custom-call | tf_op jit(solution)/shard_map/pallas_call | solution.py:133
  142.2 0.0 copy-done.4
  142.2 0.0 copy-start
  142.2 3.4 copy-done
  145.6 14.3 %shard_map.96.p_own = bf16[64,128,128]{2,1,0:T(8,128)(2,1)} custom-call(s32[64]{0:T(128)S(1)} %bitcast.46, s32[1]{0:T(128)} %bitcast.39.count, bf16[4096,2048]{1,0:T(8,128)(2,1)} %coeffs.3, bf16[2048,2048]{1,0:T(8,128)(2,1)S(1)} %copy-done), custom_call_target="tpu_custom_call" | custom-call | tf_op jit(solution)/shard_map/pallas_call | solution.py:189
  159.9 0.0 copy-start.1
  159.9 346.0 %shard_map.97 = (bf16[8,64,128,128]{3,2,1,0:T(8,128)(2,1)}, bf16[4,64,128,128]{3,2,1,0:T(8,128)(2,1)}) custom-call(bf16[64,128,128]{2,1,0:T(8,128)(2,1)} %shard_map.96.p_own, bf16[64,128,128]{2,1,0:T(8,128)(2,1)} %bitcast.44), custom_call_target="tpu_custom_call" | custom-call | tf_op jit(solution)/shard_map/pallas_call | solution.py:312
  505.9 0.0 copy-done.1
  505.9 0.0 copy-start.2
  505.9 3.4 copy-done.2
  509.3 0.0 copy-start.3
  509.3 1.6 copy-done.3
  510.9 12.6 %shard_map.98 = f32[64,128,128]{2,1,0:T(8,128)} custom-call(s32[64,128]{1,0:T(8,128)S(1)} %select_reduce_fusion.codes, s32[64]{0:T(128)S(1)} %convert_reduce_fusion.1.counts, bf16[64,128,128]{2,1,0:T(8,128)(2,1)S(1)} %copy-done.1, bf16[64,128,128]{2,1,0:T(8,128)(2,1)S(1)} %bitcast.45, bf16[8,64,128,128]{3,2,1,0:T(8,128)(2,1)} %get-tuple-element.4.p_all, ...), custom_call_target="tpu_custom_call" | custom-call | tf_op jit(solution)/shard_map/pallas_call | solution.py:368
  (8 shorter events, 0.1 us)
Async XLA Ops:
  49.7 92.5 %copy-start.4 = (s32[1,1,64]{2,1,0:T(1,128)S(1)}, s32[1,1,64]{2,1,0:T(1,128)}, u32[]{:S(2)}) copy-start(s32[1,1,64]{2,1,0:T(1,128)} %param.9) | copy-start | bytes 772
  142.2 3.4 copy-start
  159.9 346.0 %copy-start.1 = (bf16[64,128,128]{2,1,0:T(8,128)(2,1)S(1)}, bf16[64,128,128]{2,1,0:T(8,128)(2,1)}, u32[]{:S(2)}) copy-start(bf16[64,128,128]{2,1,0:T(8,128)(2,1)} %shard_map.96.p_own) | copy-start | bytes 6291460
  505.9 3.4 copy-start.2
  509.3 1.6 copy-start.3
